TPU v7x, 32 devices: a whole 2x2x4 slice. The times are simulated.
32 devices in a mesh: seq: 8 (over y, x, core), tp: 4 (over z).
Axes of the slice: x: 2, y: 2, z: 4, core: 2. Of those that a mesh axis runs over, the one named last changes fastest.
Arguments:
- queries: bfloat16 [1024, 4096], P('seq', 'tp'), may hold values from -16 to 16
- keyvalues: bfloat16 [2, 1024, 1024], P(None, 'seq', 'tp'), may hold values from -16 to 16
- stretch_order: int32 [8], replicated, may hold values from 0 to 7, each once
- block_table: int32 [8, 8], replicated, may hold values 0 or 1
- proj_weight: bfloat16 [4096, 2048], P('tp'), may hold values from -0.09375 to 0.09375
Outputs:
- projected: bfloat16 [1024, 2048], P('seq', 'tp')
Inputs may be any that keep to these rules, and one draw needn't show every extreme that they name: `stretch_order`: every stretch number 0 to 7 appears once. `block_table`: entry [i, j] matters only where j < i.
All inputs are finite; a program needn't handle non-finite values.
Results may differ from a plain program's by a relative error of at most 0.014.
Values may be sent and summed in bfloat16 or wider, within the bound.
A program may use at most 128 MiB of HBM per device.

v0:
```python
import math

import jax
import jax.numpy as jnp
from jax import lax
from jax.sharding import PartitionSpec as P

HEAD_SIZE = 128


def per_device(queries, keyvalues, stretch_order, block_table, proj_weight):
    shard_rows = queries.shape[0]
    kv_width = keyvalues.shape[2]
    kv_heads = kv_width // HEAD_SIZE
    q_heads = queries.shape[1] // HEAD_SIZE
    group_width = q_heads // kv_heads
    stretch_total = stretch_order.shape[0]
    score_scale = 1.0 / HEAD_SIZE**0.5
    my_index = lax.axis_index("seq")
    my_stretch = stretch_order[my_index]
    table_row = block_table[my_stretch]
    query_pos = my_stretch * shard_rows + jnp.arange(shard_rows, dtype=jnp.int32)
    query_four = queries.reshape(shard_rows, kv_heads, group_width, HEAD_SIZE)
    stretch_ids = jnp.arange(stretch_total, dtype=jnp.int32)

    def attend(carried, key_matrix, value_matrix, key_stretches):
        row_count = key_matrix.shape[0]
        key_pos = key_stretches * shard_rows + jnp.arange(row_count, dtype=jnp.int32) % shard_rows
        table_hits = jnp.sum(
            jnp.where(key_stretches[:, None] == stretch_ids[None, :], table_row[None, :], 0), axis=1
        )
        same_stretch = (key_stretches[None, :] == my_stretch) & (
            key_pos[None, :] <= query_pos[:, None]
        )
        earlier = (key_stretches[None, :] < my_stretch) & (table_hits[None, :] == 1)
        allowed = same_stretch | earlier
        scores = (
            jnp.einsum(
                "tkgd,skd->kgts",
                query_four,
                key_matrix.reshape(row_count, kv_heads, HEAD_SIZE),
                preferred_element_type=jnp.float32,
            )
            * score_scale
        )
        scores = jnp.where(allowed, scores, -1e30)
        running_max, denominator, numerator = carried
        new_max = jnp.maximum(running_max, jnp.max(scores, axis=-1))
        weights = jnp.where(allowed, jnp.exp(scores - new_max[..., None]), 0.0)
        factor = jnp.exp(running_max - new_max)
        denominator = denominator * factor + jnp.sum(weights, axis=-1)
        numerator = numerator * factor[..., None] + jnp.einsum(
            "kgts,skd->kgtd",
            weights.astype(jnp.bfloat16),
            value_matrix.reshape(row_count, kv_heads, HEAD_SIZE),
            preferred_element_type=jnp.float32,
        )
        return (new_max, denominator, numerator)

    start_state = (
        jnp.full((kv_heads, group_width, shard_rows), -1e30, jnp.float32),
        jnp.zeros((kv_heads, group_width, shard_rows), jnp.float32),
        jnp.zeros((kv_heads, group_width, shard_rows, HEAD_SIZE), jnp.float32),
    )
    key_matrix = lax.all_gather(keyvalues[0], "seq", axis=0, tiled=True)
    value_matrix = lax.all_gather(keyvalues[1], "seq", axis=0, tiled=True)
    shard_count = key_matrix.shape[0] // shard_rows
    grouped = math.gcd(shard_count, max(1, 512 // shard_rows))
    span_rows = shard_rows * grouped

    def many_shards(block_index, inner):
        sources = block_index * grouped + jnp.arange(span_rows, dtype=jnp.int32) // shard_rows
        stretches = jnp.sum(
            jnp.where(sources[:, None] == stretch_ids[None, :], stretch_order[None, :], 0), axis=1
        )
        block_keys = lax.dynamic_slice_in_dim(key_matrix, block_index * span_rows, span_rows, 0)
        block_values = lax.dynamic_slice_in_dim(value_matrix, block_index * span_rows, span_rows, 0)
        return attend(inner, block_keys, block_values, stretches)

    final = lax.fori_loop(0, shard_count // grouped, many_shards, start_state)
    running_max, denominator, numerator = final
    attended = numerator / denominator[..., None]
    attended = (
        jnp.transpose(attended, (2, 0, 1, 3))
        .reshape(shard_rows, q_heads * HEAD_SIZE)
        .astype(jnp.bfloat16)
    )
    partial_sums = jnp.dot(attended, proj_weight, preferred_element_type=jnp.float32)
    return lax.psum_scatter(
        partial_sums.astype(jnp.bfloat16), "tp", scatter_dimension=1, tiled=True
    )


def solution(mesh):
    in_specs = (P("seq", "tp"), P(None, "seq", "tp"), P(), P(), P("tp", None))
    out_specs = P("seq", "tp")
    return jax.shard_map(
        per_device, mesh=mesh, in_specs=in_specs, out_specs=out_specs, check_vma=False
    )
```

profile of v0, /device:TPU:0, one launch (start us, length us, event | category | flops | bytes accessed | tf_op | source)
XLA Modules:
  0.0 74.4 jit_solution(7622967360517775287)
XLA Ops:
  6.5 1.4 %dynamic_slice.26 = s32[1]{0:T(128)} dynamic-slice(s32[8]{0:T(128)} %param.9, s32[]{:T(128)S(6)} %select_n.99), dynamic_slice_sizes={1} | dynamic-slice | bytes 12 | tf_op jit(solution)/shard_map/dynamic_slice | solution.py:20
  10.0 0.9 %fusion.25 = (bf16[1,128,256]{2,1,0:T(8,128)(2,1)S(1)}, bf16[1,128,256]{2,1,0:T(8,128)(2,1)S(1)}) fusion(bf16[2,128,256]{2,1,0:T(8,128)(2,1)} %param.8), kind=kLoop, calls=%fused_computation.46 | loop fusion | bytes 262144 | tf_op jit(solution)/shard_map/slice | solution.py:66
  10.9 0.1 copy.31
  11.0 0.1 copy.30
  11.2 1.1 %copy.19 = bf16[128,1024]{0,1:T(8,128)(2,1)S(1)} copy(bf16[128,1024]{1,0:T(8,128)(2,1)} %param.7) | data formatting | bytes 524288 | tf_op args[0]
  12.3 0.2 copy.21
  12.5 11.5 %all-gather = bf16[1,1024,256]{1,2,0:T(8,128)(2,1)S(1)} all-gather(bf16[1,128,256]{1,2,0:T(8,128)(2,1)S(1)} %copy.30), channel_id=2, replica_groups=mesh['seq'=8,'tp'=4] {'seq'}, dimensions={1}, use_global_device_ids=true | all-gather | bytes 589824 | tf_op jit(solution)/shard_map/all_gather | solution.py:65
  23.9 9.9 %all-gather.1 = bf16[1,1024,256]{1,2,0:T(8,128)(2,1)S(1)} all-gather(bf16[1,128,256]{1,2,0:T(8,128)(2,1)S(1)} %copy.31), channel_id=3, replica_groups=mesh['seq'=8,'tp'=4] {'seq'}, dimensions={1}, use_global_device_ids=true | all-gather | bytes 589824 | tf_op jit(solution)/shard_map/all_gather | solution.py:66
  34.6 6.6 %while.21 = (s32[]{:T(128)}, f32[2,4,128]{2,1,0:T(4,128)S(1)}, f32[2,4,128]{2,1,0:T(4,128)S(1)}, f32[2,4,128,128]{3,2,1,0:T(8,128)S(1)}, s32[8]{0:T(128)S(1)}, /...) while((s32[]{:T(128)}, f32[2,4,128]{2,1,0:T(4,128)S(1)}, ...), condition=%wide.region_5.6_spmd.clone.clone, body=%wide.region_0.5_spmd.clone.clone.sunk | while | flops 275880576 | bytes 9526579 | solution.py:80
  34.8 0.1 select_reduce_fusion.5
  34.8 0.7 broadcast_compare_fusion.2
  35.5 0.3 and_or_fusion.2
  35.9 0.5 fusion.46
  36.4 0.5 fusion.47
  37.0 0.9 %convolution_add_fusion.2 = f32[2,4,128,128]{3,2,1,0:T(8,128)S(1)} fusion(bf16[512,2,128,1]{0,2,3,1:T(8,128)(2,1)S(1)} %bitcast.53, f32[2,512,128,4]{2,1,3,0:T(8,128)S(1)} %get-tuple-element.502, f32[2,4,128]{2,1,0:T(4,128)S(1)} %select_maximum_fusion.2, pred[128,512]{0,1:T(8,128)(4,1)S(1)} %and_or_fusion.2, ...), kind=kOutput, calls=%fused_computation.7.clone.1 | convolution fusion | flops 137232384 | bytes 3481601 | tf_op jit(solution)/shard_map/while/body/eval_jaxpr/kgts,skd->kgtd/dot_general | solution.py:52
  38.1 0.1 select_reduce_fusion.5
  38.2 0.7 broadcast_compare_fusion.2
  38.9 0.3 and_or_fusion.2
  39.2 0.5 fusion.46
  39.8 0.5 fusion.47
  40.3 0.9 %convolution_add_fusion.2 = f32[2,4,128,128]{3,2,1,0:T(8,128)S(1)} fusion(bf16[512,2,128,1]{0,2,3,1:T(8,128)(2,1)S(1)} %bitcast.53, f32[2,512,128,4]{2,1,3,0:T(8,128)S(1)} %get-tuple-element.502, f32[2,4,128]{2,1,0:T(4,128)S(1)} %select_maximum_fusion.2, pred[128,512]{0,1:T(8,128)(4,1)S(1)} %and_or_fusion.2, ...), kind=kOutput, calls=%fused_computation.7.clone.1 | convolution fusion | flops 137232384 | bytes 3481601 | tf_op jit(solution)/shard_map/while/body/eval_jaxpr/kgts,skd->kgtd/dot_general | solution.py:52
  41.3 0.2 copy.22
  41.5 3.7 %convolution_convert_fusion = bf16[128,2048]{1,0:T(8,128)(2,1)} fusion(bf16[128,1024]{0,1:T(8,128)(2,1)S(1)} %bitcast.56, bf16[1024,2048]{1,0:T(8,128)(2,1)} %param.11), kind=kOutput, calls=%fused_computation.43 | convolution fusion | flops 537133056 | bytes 4980736 | tf_op jit(solution)/shard_map/dot_general | solution.py:88
  45.3 22.3 %reduce-scatter.2.cloned.1.call-done = bf16[128,512]{1,0:T(8,128)(2,1)} async-done(((bf16[128,2048]{1,0:T(8,128)(2,1)}), bf16[128,512]{1,0:T(8,128)(2,1)}) %reduce-scatter.2.cloned.1.call-update) | async-done | bytes 131088 | tf_op jit(solution)/shard_map/reduce_scatter | solution.py:89
  (27 shorter events, 0.4 us)
Async XLA Ops:
  6.5 28.0 %copy-start = (s32[8,8]{1,0:T(8,128)S(1)}, s32[8,8]{1,0:T(8,128)}, u32[]{:S(2)}) copy-start(s32[8,8]{1,0:T(8,128)} %param.10) | copy-start | bytes 772
  6.5 28.1 %copy-start.1 = (s32[8]{0:T(128)S(1)}, s32[8]{0:T(128)}, u32[]{:S(2)}) copy-start(s32[8]{0:T(128)} %param.9) | copy-start | bytes 100
  6.5 61.0 %reduce-scatter.2.cloned.1.call-start = ((), (), s32[]{:S(2)}) async-start(), calls=%async_computation.1 | async-start | bytes 655360 | tf_op jit(solution)/shard_map/reduce_scatter | solution.py:89
Sparse Core Ops, SparseCore 0:
  45.4 22.0 reduce-scatter.1
where the time goes:
time: 74.7 us; the launch traced here: 74.4 us
  waiting for transfers between devices  22.3 us (30%)
  blocking collectives  21.4 us (29%)
  between operations  16.3 us (22%)
  matrix products  6.69 us (9%)
  local copies, waits for them, and re-layouts  4.12 us (6%)
  other arithmetic  3.46 us (5%)
    reduce_scatter x1, waiting for transfers between devices, per_device(): lax.psum_scatter(partial_sums.astype(jnp.bfloat16), 'tp', scatter_dimensi...  22.3 us
    all_gather x1, blocking collectives, per_device(): key_matrix = lax.all_gather(keyvalues[0], 'seq', axis=0, tiled=True)  11.5 us
    all_gather x1, blocking collectives, per_device(): value_matrix = lax.all_gather(keyvalues[1], 'seq', axis=0, tiled=True)  9.94 us
    dot_general x1, matrix products, per_device(): jnp.dot(attended, proj_weight, preferred_element_type=jnp.float32)  3.72 us
    dot_general x2, matrix products, attend(): jnp.einsum('kgts,skd->kgtd', weights.astype(jnp.bfloat16), value_matrix.r...  1.89 us
    unnamed x8, local copies, waits for them, and re-layouts  1.55 us
  transfers between devices with their start and end apart: 1, of which 1 were waited for; matrix products, arithmetic and copies ran while one was open for 0% of the time, Pallas kernels for 0%

commit v1 on v0

v1 whole, which is shorter than its diff:
```python
import functools

import jax
import jax.numpy as jnp
from jax import lax
from jax.experimental import pallas as pl
from jax.experimental.pallas import tpu as pltpu
from jax.sharding import PartitionSpec as P

HEAD = 128
MASKED = -1e30
LOG2E = 1.4426950408889634
MESH = pl.DeviceIdType.MESH


def kernel(
    n, tp, q_hbm, kv_hbm, order, table, w_hbm, out_ref,
    q_in, q_rows, k_buf, v_buf, w_buf, run_max, acc, att, parts, got,
    in_sem, k_send, v_send, k_recv, v_recv, k_fwd, v_fwd, p_send, p_recv,
):
    rows = q_in.shape[0]
    kv_heads = k_buf.shape[1] // HEAD
    q_heads = q_in.shape[1] // HEAD
    group = q_heads // kv_heads
    grows = group * rows
    width = got.shape[2]
    chips = n // 2
    me = lax.axis_index("seq")
    mt = lax.axis_index("tp")
    chip = me // 2
    core = me % 2
    partner = chip * 2 + 1 - core

    def slot(ref, s, count=1):
        return ref.at[pl.ds(pl.multiple_of(s * rows, rows), count * rows)]

    own_k = pltpu.make_async_copy(kv_hbm.at[0], slot(k_buf, me), in_sem.at[0])
    own_v = pltpu.make_async_copy(kv_hbm.at[1], slot(v_buf, me), in_sem.at[1])
    load_q = pltpu.make_async_copy(q_hbm, q_in, in_sem.at[2])
    load_w = pltpu.make_async_copy(w_hbm, w_buf, in_sem.at[3])
    own_k.start()
    own_v.start()
    load_q.start()

    barrier = pltpu.get_barrier_semaphore()

    def peer(j):
        return ((chip + j) % chips) * 2 + core

    def each(lo, hi, body):
        if hi - lo <= 8:
            for j in range(lo, hi):
                body(j)
        else:
            lax.fori_loop(lo, hi, lambda j, c: (body(j), c)[1], 0)

    def greet_seq(s):
        pl.semaphore_signal(barrier, inc=1, device_id={"seq": s}, device_id_type=MESH)

    greet_seq(partner)
    each(1, chips, lambda j: greet_seq(peer(j)))
    for j in range(1, tp):
        pl.semaphore_signal(barrier, inc=1, device_id={"tp": (mt + j) % tp}, device_id_type=MESH)

    own_k.wait()
    own_v.wait()
    pl.semaphore_wait(barrier, 1 + (chips - 1) + (tp - 1))

    def remote(buf, s, send, recv, index, target):
        return pltpu.make_async_remote_copy(
            src_ref=slot(buf, s), dst_ref=slot(buf, s),
            send_sem=send.at[index], recv_sem=recv.at[s],
            device_id={"seq": target}, device_id_type=MESH,
        )

    def send_all(j):
        remote(k_buf, me, k_send, k_recv, j, peer(j)).start()
        remote(v_buf, me, v_send, v_recv, j, peer(j)).start()

    remote(k_buf, me, k_fwd, k_recv, 0, partner).start()
    remote(v_buf, me, v_fwd, v_recv, 0, partner).start()
    each(1, chips, send_all)
    load_w.start()

    my_stretch = order[me]
    load_q.wait()
    for h in range(q_heads):
        q_rows[h * rows:(h + 1) * rows, :] = q_in[:, h * HEAD:(h + 1) * HEAD]

    def bias_of(s):
        key_stretch = order[s]
        seen = jnp.logical_and(key_stretch < my_stretch, table[my_stretch, key_stretch] == 1)
        return jnp.where(seen, 0.0, MASKED).astype(jnp.float32)

    lane = lax.broadcasted_iota(jnp.int32, (1, 2 * rows), 1)
    scale = LOG2E / HEAD**0.5

    def attend(pair, first):
        bias = jnp.where(lane < rows, bias_of(pair * 2), bias_of(pair * 2 + 1))
        start = pl.multiple_of(pair * 2 * rows, 2 * rows)
        for g in range(kv_heads):
            cols = slice(g * HEAD, (g + 1) * HEAD)
            here = slice(g * grows, (g + 1) * grows)
            keys = k_buf[pl.ds(start, 2 * rows), cols]
            values = v_buf[pl.ds(start, 2 * rows), cols]
            scores = lax.dot_general(
                q_rows[here, :], keys, (((1,), (1,)), ((), ())),
                preferred_element_type=jnp.float32,
            )
            if first:
                q_pos = lax.broadcasted_iota(jnp.int32, (grows, 2 * rows), 0) % rows
                k_col = lax.broadcasted_iota(jnp.int32, (grows, 2 * rows), 1)
                k_pos = k_col - core * rows
                own = (k_pos >= 0) & (k_pos < rows)
                scores = jnp.where(
                    own, jnp.where(k_pos <= q_pos, scores, MASKED), scores + bias
                )
            else:
                scores = scores + bias
            top = jnp.max(scores, axis=1, keepdims=True)
            if first:
                new_max = top
            else:
                old_max = run_max[here, 0:1]
                new_max = jnp.maximum(old_max, top)
            weights = jnp.exp2((scores - new_max) * scale).astype(jnp.bfloat16)
            wide = jnp.concatenate([values, jnp.ones_like(values)], axis=1)
            added = jnp.dot(weights, wide, preferred_element_type=jnp.float32)
            if first:
                acc[here, :] = added
            else:
                acc[here, :] = acc[here, :] * jnp.exp2((old_max - new_max) * scale) + added
            run_max[here, :] = jnp.broadcast_to(new_max, (grows, HEAD))

    def wait_slot(s):
        remote(k_buf, s, k_fwd, k_recv, 0, partner).wait_recv()
        remote(v_buf, s, v_fwd, v_recv, 0, partner).wait_recv()

    wait_slot(partner)
    attend(chip, True)

    def step(j):
        s = ((chip - j + chips) % chips) * 2 + core
        other = ((chip - j + chips) % chips) * 2 + 1 - core
        remote(k_buf, s, k_fwd, k_recv, j, partner).wait_recv()
        remote(k_buf, s, k_fwd, k_recv, j, partner).start()
        remote(v_buf, s, v_fwd, v_recv, j, partner).wait_recv()
        remote(v_buf, s, v_fwd, v_recv, j, partner).start()
        wait_slot(other)
        attend((chip - j + chips) % chips, False)

    each(1, chips, step)

    for h in range(q_heads):
        here = slice(h * rows, (h + 1) * rows)
        att[:, h * HEAD:(h + 1) * HEAD] = (
            acc[here, :HEAD] / acc[here, HEAD:]
        ).astype(jnp.bfloat16)

    load_w.wait()

    def project(t):
        return jnp.dot(
            att[...], w_buf[:, pl.ds(pl.multiple_of(t * width, width), width)],
            preferred_element_type=jnp.float32,
        )

    def part_copy(j, source, target):
        return pltpu.make_async_remote_copy(
            src_ref=parts.at[j], dst_ref=got.at[source],
            send_sem=p_send.at[j], recv_sem=p_recv.at[source],
            device_id={"tp": target}, device_id_type=MESH,
        )

    ahead = sorted(range(1, tp), key=lambda j: -min(j, tp - j))
    for j in ahead:
        t = (mt + j) % tp
        parts[j] = project(t).astype(jnp.bfloat16)
        part_copy(j, mt, t).start()
    total = project(mt)
    for j in reversed(ahead):
        source = (mt + j) % tp
        part_copy(j, source, source).wait_recv()
        total = total + got[source].astype(jnp.float32)
    out_ref[...] = total.astype(out_ref.dtype)

    def drain(j):
        remote(k_buf, me, k_send, k_recv, j, peer(j)).wait_send()
        remote(v_buf, me, v_send, v_recv, j, peer(j)).wait_send()

    def drain_fwd(j):
        remote(k_buf, me, k_fwd, k_recv, j, partner).wait_send()
        remote(v_buf, me, v_fwd, v_recv, j, partner).wait_send()

    each(1, chips, drain)
    each(0, chips, drain_fwd)
    for j in ahead:
        part_copy(j, mt, (mt + j) % tp).wait_send()


def solution(mesh):
    n, tp = mesh.shape["seq"], mesh.shape["tp"]

    def per_device(queries, keyvalues, stretch_order, block_table, proj_weight):
        rows, q_width = queries.shape
        kv_width = keyvalues.shape[2]
        dout = proj_weight.shape[1]
        q_heads = q_width // HEAD
        dma = pltpu.SemaphoreType.DMA
        return pl.pallas_call(
            functools.partial(kernel, n, tp),
            out_shape=jax.ShapeDtypeStruct((rows, dout // tp), jnp.bfloat16),
            in_specs=[
                pl.BlockSpec(memory_space=pl.ANY),
                pl.BlockSpec(memory_space=pl.ANY),
                pl.BlockSpec(memory_space=pltpu.SMEM),
                pl.BlockSpec(memory_space=pltpu.SMEM),
                pl.BlockSpec(memory_space=pl.ANY),
            ],
            out_specs=pl.BlockSpec(memory_space=pltpu.VMEM),
            scratch_shapes=[
                pltpu.VMEM((rows, q_width), jnp.bfloat16),
                pltpu.VMEM((q_heads * rows, HEAD), jnp.bfloat16),
                pltpu.VMEM((n * rows, kv_width), jnp.bfloat16),
                pltpu.VMEM((n * rows, kv_width), jnp.bfloat16),
                pltpu.VMEM(proj_weight.shape, jnp.bfloat16),
                pltpu.VMEM((q_heads * rows, HEAD), jnp.float32),
                pltpu.VMEM((q_heads * rows, 2 * HEAD), jnp.float32),
                pltpu.VMEM((rows, q_width), jnp.bfloat16),
                pltpu.VMEM((tp, rows, dout // tp), jnp.bfloat16),
                pltpu.VMEM((tp, rows, dout // tp), jnp.bfloat16),
                dma((4,)),
                dma((n // 2,)), dma((n // 2,)),
                dma((n,)), dma((n,)),
                dma((n // 2,)), dma((n // 2,)),
                dma((tp,)), dma((tp,)),
            ],
            compiler_params=pltpu.CompilerParams(collective_id=0, has_side_effects=True),
        )(queries, keyvalues, stretch_order, block_table, proj_weight)

    return jax.shard_map(
        per_device, mesh=mesh,
        in_specs=(P("seq", "tp"), P(None, "seq", "tp"), P(), P(), P("tp", None)),
        out_specs=P("seq", "tp"), check_vma=False,
    )
```

time: 74.7 us -> 34.7 us (0.46)
  the two profiles are of different devices: /device:TPU:0 before, /device:TPU:17 now
where the time goes in v1:
time: 34.7 us; the launch traced here: 34.5 us
  Pallas kernels  32.9 us (95%)
  local copies, waits for them, and re-layouts  1.57 us (5%)
    pallas_call x1, Pallas kernels, per_device(): pl.pallas_call(functools.partial(kernel, n, tp), out_shape=jax.ShapeDtype...  32.9 us
    unnamed x1, local copies, waits for them, and re-layouts  1.57 us

profile of v1, /device:TPU:17, one launch (start us, length us, event | category | flops | bytes accessed | tf_op | source)
XLA Modules:
  0.0 34.5 jit_solution(8541190720569104648)
XLA Ops:
  0.0 32.9 %shard_map.55 = bf16[128,512]{1,0:T(8,128)(2,1)} custom-call(bf16[128,1024]{1,0:T(8,128)(2,1)} %q_hbm.1, bf16[2,128,256]{2,1,0:T(8,128)(2,1)} %kv_hbm.1, s32[8]{0:T(128)} %order.1, s32[8,8]{1,0:T(8,128)} %table.1, bf16[1024,2048]{1,0:T(8,128)(2,1)} %w_hbm.1), custom_call_target="tpu_custom_call" | custom-call | tf_op jit(solution)/shard_map/pallas_call | solution.py:210
  32.9 1.6 %copy.7 = bf16[128,512]{1,0:T(8,128)(2,1)} copy(bf16[128,512]{1,0:T(8,128)(2,1)} %shard_map.55) | data formatting | bytes 262144

commit v2 on v1

--- a/solution.py
+++ b/solution.py
@@ -15,8 +15,8 @@
 
 def kernel(
     n, tp, q_hbm, kv_hbm, order, table, w_hbm, out_ref,
-    q_in, q_rows, k_buf, v_buf, w_buf, run_max, acc, att, parts, got,
-    in_sem, k_send, v_send, k_recv, v_recv, k_fwd, v_fwd, p_send, p_recv,
+    q_in, q_rows, k_buf, v_buf, w_buf, run_max, acc, att, parts, got, relay,
+    in_sem, k_send, v_send, k_recv, v_recv, k_fwd, v_fwd, p_send, p_recv, r_recv,
 ):
     rows = q_in.shape[0]
     kv_heads = k_buf.shape[1] // HEAD
@@ -41,6 +41,7 @@
     own_k.start()
     own_v.start()
     load_q.start()
+    load_w.start()
 
     barrier = pltpu.get_barrier_semaphore()
 
@@ -57,14 +58,46 @@
     def greet_seq(s):
         pl.semaphore_signal(barrier, inc=1, device_id={"seq": s}, device_id_type=MESH)
 
+    def greet_tp(t):
+        pl.semaphore_signal(barrier, inc=1, device_id={"tp": t}, device_id_type=MESH)
+
+    square = chips == 4
+    chip_x, chip_y = chip % 2, chip // 2
+    xn = (chip_y * 2 + 1 - chip_x) * 2 + core
+    yn = ((1 - chip_y) * 2 + chip_x) * 2 + core
+    dn = ((1 - chip_y) * 2 + 1 - chip_x) * 2 + core
+    line = tp == 4
+    side = mt // 2
+    inner = mt % 2 * (1 - side) + (1 - mt % 2) * side
+
+    def mirror(d):
+        return d * (1 - side) + (3 - d) * side
+
     greet_seq(partner)
-    each(1, chips, lambda j: greet_seq(peer(j)))
-    for j in range(1, tp):
-        pl.semaphore_signal(barrier, inc=1, device_id={"tp": (mt + j) % tp}, device_id_type=MESH)
+    if square:
+        greet_seq(xn)
+        greet_seq(yn)
+        seq_peers = 3
+    else:
+        each(1, chips, lambda j: greet_seq(peer(j)))
+        seq_peers = chips
+    if line:
+        greet_tp(mirror(2))
+        greet_tp(mirror(1 - inner))
+
+        @pl.when(inner == 1)
+        def _():
+            greet_tp(mirror(3))
+
+        tp_peers = 2 + inner
+    else:
+        for j in range(1, tp):
+            greet_tp((mt + j) % tp)
+        tp_peers = tp - 1
 
     own_k.wait()
     own_v.wait()
-    pl.semaphore_wait(barrier, 1 + (chips - 1) + (tp - 1))
+    pl.semaphore_wait(barrier, seq_peers + tp_peers)
 
     def remote(buf, s, send, recv, index, target):
         return pltpu.make_async_remote_copy(
@@ -79,8 +112,13 @@
 
     remote(k_buf, me, k_fwd, k_recv, 0, partner).start()
     remote(v_buf, me, v_fwd, v_recv, 0, partner).start()
-    each(1, chips, send_all)
-    load_w.start()
+    if square:
+        remote(k_buf, me, k_send, k_recv, 0, xn).start()
+        remote(v_buf, me, v_send, v_recv, 0, yn).start()
+        remote(v_buf, me, v_send, v_recv, 1, xn).start()
+        remote(k_buf, me, k_send, k_recv, 1, yn).start()
+    else:
+        each(1, chips, send_all)
 
     my_stretch = order[me]
     load_q.wait()
@@ -95,14 +133,17 @@
     lane = lax.broadcasted_iota(jnp.int32, (1, 2 * rows), 1)
     scale = LOG2E / HEAD**0.5
 
-    def attend(pair, first):
-        bias = jnp.where(lane < rows, bias_of(pair * 2), bias_of(pair * 2 + 1))
-        start = pl.multiple_of(pair * 2 * rows, 2 * rows)
+    def attend(first_slot, count, first):
+        if count == 2:
+            bias = jnp.where(lane < rows, bias_of(first_slot), bias_of(first_slot + 1))
+        else:
+            bias = bias_of(first_slot)
+        start = pl.multiple_of(first_slot * rows, rows)
         for g in range(kv_heads):
             cols = slice(g * HEAD, (g + 1) * HEAD)
             here = slice(g * grows, (g + 1) * grows)
-            keys = k_buf[pl.ds(start, 2 * rows), cols]
-            values = v_buf[pl.ds(start, 2 * rows), cols]
+            keys = k_buf[pl.ds(start, count * rows), cols]
+            values = v_buf[pl.ds(start, count * rows), cols]
             scores = lax.dot_general(
                 q_rows[here, :], keys, (((1,), (1,)), ((), ())),
                 preferred_element_type=jnp.float32,
@@ -137,7 +178,7 @@
         remote(v_buf, s, v_fwd, v_recv, 0, partner).wait_recv()
 
     wait_slot(partner)
-    attend(chip, True)
+    attend(chip * 2, 2, True)
 
     def step(j):
         s = ((chip - j + chips) % chips) * 2 + core
@@ -147,9 +188,30 @@
         remote(v_buf, s, v_fwd, v_recv, j, partner).wait_recv()
         remote(v_buf, s, v_fwd, v_recv, j, partner).start()
         wait_slot(other)
-        attend((chip - j + chips) % chips, False)
-
-    each(1, chips, step)
+        attend(s - core, 2, False)
+
+    def arrive(buf, recv, fwd, s, j, onward=None, send=None):
+        remote(buf, s, fwd, recv, j, partner).wait_recv()
+        if onward is not None:
+            remote(buf, s, send, recv, 2, onward).start()
+        remote(buf, s, fwd, recv, j, partner).start()
+
+    if square:
+        arrive(k_buf, k_recv, k_fwd, xn, 1, yn, k_send)
+        arrive(v_buf, v_recv, v_fwd, yn, 2, xn, v_send)
+        arrive(v_buf, v_recv, v_fwd, xn, 1)
+        arrive(k_buf, k_recv, k_fwd, yn, 2)
+        wait_slot(xn + 1 - 2 * core)
+        attend(xn - core, 2, False)
+        wait_slot(yn + 1 - 2 * core)
+        attend(yn - core, 2, False)
+        arrive(k_buf, k_recv, k_fwd, dn, 3)
+        arrive(v_buf, v_recv, v_fwd, dn, 3)
+        attend(dn, 1, False)
+        wait_slot(dn + 1 - 2 * core)
+        attend(dn + 1 - 2 * core, 1, False)
+    else:
+        each(1, chips, step)
 
     for h in range(q_heads):
         here = slice(h * rows, (h + 1) * rows)
@@ -172,17 +234,70 @@
             device_id={"tp": target}, device_id_type=MESH,
         )
 
-    ahead = sorted(range(1, tp), key=lambda j: -min(j, tp - j))
-    for j in ahead:
-        t = (mt + j) % tp
-        parts[j] = project(t).astype(jnp.bfloat16)
-        part_copy(j, mt, t).start()
-    total = project(mt)
-    for j in reversed(ahead):
-        source = (mt + j) % tp
-        part_copy(j, source, source).wait_recv()
-        total = total + got[source].astype(jnp.float32)
-    out_ref[...] = total.astype(out_ref.dtype)
+    def half_copy(i, dst, recv, target):
+        piece = pl.ds(i * (rows // 2), rows // 2)
+        return pltpu.make_async_remote_copy(
+            src_ref=parts.at[2, piece], dst_ref=dst.at[piece],
+            send_sem=p_send.at[2 + i], recv_sem=recv,
+            device_id={"tp": target}, device_id_type=MESH,
+        )
+
+    if line:
+        m0, m1, m2, m3 = (mirror(d) for d in range(4))
+
+        @pl.when(inner == 0)
+        def _():
+            parts[2] = project(m3).astype(jnp.bfloat16)
+            for i in range(2):
+                half_copy(i, relay, r_recv.at[i], m1).start()
+            parts[0] = project(m2).astype(jnp.bfloat16)
+            part_copy(0, mt, m2).start()
+            parts[1] = project(m1).astype(jnp.bfloat16)
+            part_copy(1, mt, m1).start()
+            total = project(mt)
+            part_copy(0, m1, m1).wait_recv()
+            total = total + got[m1].astype(jnp.float32)
+            for i in range(2):
+                half_copy(i, got.at[m2], r_recv.at[i], m2).wait_recv()
+            total = total + got[m2].astype(jnp.float32)
+            out_ref[...] = total.astype(out_ref.dtype)
+
+        @pl.when(inner == 1)
+        def _():
+            parts[0] = project(m2).astype(jnp.bfloat16)
+            part_copy(0, mt, m2).start()
+            parts[1] = project(m0).astype(jnp.bfloat16)
+            part_copy(1, mt, m0).start()
+            far = project(m3)
+            total = project(mt)
+            for i in range(2):
+                piece = slice(i * (rows // 2), (i + 1) * (rows // 2))
+                half_copy(i, relay, r_recv.at[i], m0).wait_recv()
+                parts[2, piece] = (far[piece] + relay[piece].astype(jnp.float32)).astype(jnp.bfloat16)
+                half_copy(i, got.at[mt], r_recv.at[i], m3).start()
+            for source in (m2, m3, m0):
+                part_copy(0, source, source).wait_recv()
+                total = total + got[source].astype(jnp.float32)
+            out_ref[...] = total.astype(out_ref.dtype)
+
+        part_copy(0, mt, m2).wait_send()
+        part_copy(1, mt, m0).wait_send()
+        for i in range(2):
+            half_copy(i, relay, r_recv.at[i], m1).wait_send()
+    else:
+        ahead = sorted(range(1, tp), key=lambda j: -min(j, tp - j))
+        for j in ahead:
+            t = (mt + j) % tp
+            parts[j] = project(t).astype(jnp.bfloat16)
+            part_copy(j, mt, t).start()
+        total = project(mt)
+        for j in reversed(ahead):
+            source = (mt + j) % tp
+            part_copy(j, source, source).wait_recv()
+            total = total + got[source].astype(jnp.float32)
+        out_ref[...] = total.astype(out_ref.dtype)
+        for j in ahead:
+            part_copy(j, mt, (mt + j) % tp).wait_send()
 
     def drain(j):
         remote(k_buf, me, k_send, k_recv, j, peer(j)).wait_send()
@@ -192,10 +307,13 @@
         remote(k_buf, me, k_fwd, k_recv, j, partner).wait_send()
         remote(v_buf, me, v_fwd, v_recv, j, partner).wait_send()
 
-    each(1, chips, drain)
+    if square:
+        for j in range(3):
+            remote(k_buf, me, k_send, k_recv, j, yn).wait_send()
+            remote(v_buf, me, v_send, v_recv, j, xn).wait_send()
+    else:
+        each(1, chips, drain)
     each(0, chips, drain_fwd)
-    for j in ahead:
-        part_copy(j, mt, (mt + j) % tp).wait_send()
 
 
 def solution(mesh):
@@ -229,11 +347,12 @@
                 pltpu.VMEM((rows, q_width), jnp.bfloat16),
                 pltpu.VMEM((tp, rows, dout // tp), jnp.bfloat16),
                 pltpu.VMEM((tp, rows, dout // tp), jnp.bfloat16),
+                pltpu.VMEM((rows, dout // tp), jnp.bfloat16),
                 dma((4,)),
                 dma((n // 2,)), dma((n // 2,)),
                 dma((n,)), dma((n,)),
                 dma((n // 2,)), dma((n // 2,)),
-                dma((tp,)), dma((tp,)),
+                dma((max(tp, 4),)), dma((tp,)), dma((2,)),
             ],
             compiler_params=pltpu.CompilerParams(collective_id=0, has_side_effects=True),
         )(queries, keyvalues, stretch_order, block_table, proj_weight)

time: 34.7 us -> 31.5 us (0.908)
  the two profiles are of different devices: /device:TPU:17 before, /device:TPU:0 now
where the time goes in v2:
time: 31.5 us; the launch traced here: 31.3 us
  Pallas kernels  29.7 us (94%)
  local copies, waits for them, and re-layouts  1.57 us (5%)
    pallas_call x1, Pallas kernels, per_device(): pl.pallas_call(functools.partial(kernel, n, tp), out_shape=jax.ShapeDtype...  29.7 us
    unnamed x1, local copies, waits for them, and re-layouts  1.57 us

profile of v2, /device:TPU:0, one launch (start us, length us, event | category | flops | bytes accessed | tf_op | source)
XLA Modules:
  0.0 31.3 jit_solution(13740990611187651763)
XLA Ops:
  0.0 29.7 %shard_map.55 = bf16[128,512]{1,0:T(8,128)(2,1)} custom-call(bf16[128,1024]{1,0:T(8,128)(2,1)} %q_hbm.1, bf16[2,128,256]{2,1,0:T(8,128)(2,1)} %kv_hbm.1, s32[8]{0:T(128)} %order.1, s32[8,8]{1,0:T(8,128)} %table.1, bf16[1024,2048]{1,0:T(8,128)(2,1)} %w_hbm.1), custom_call_target="tpu_custom_call" | custom-call | tf_op jit(solution)/shard_map/pallas_call | solution.py:328
  29.7 1.6 %copy.7 = bf16[128,512]{1,0:T(8,128)(2,1)} copy(bf16[128,512]{1,0:T(8,128)(2,1)} %shard_map.55) | data formatting | bytes 262144

commit v3 on v2

--- a/solution.py
+++ b/solution.py
@@ -14,8 +14,8 @@
 
 
 def kernel(
-    n, tp, q_hbm, kv_hbm, order, table, w_hbm, out_ref,
-    q_in, q_rows, k_buf, v_buf, w_buf, run_max, acc, att, parts, got, relay,
+    n, tp, q_hbm, kv_hbm, order_hbm, table_hbm, w_hbm, out_ref,
+    order, table, q_in, q_rows, k_buf, v_buf, w_buf, run_max, acc, att, parts, got, relay,
     in_sem, k_send, v_send, k_recv, v_recv, k_fwd, v_fwd, p_send, p_recv, r_recv,
 ):
     rows = q_in.shape[0]
@@ -41,6 +41,10 @@
     own_k.start()
     own_v.start()
     load_q.start()
+    load_order = pltpu.make_async_copy(order_hbm, order, in_sem.at[4])
+    load_table = pltpu.make_async_copy(table_hbm, table, in_sem.at[5])
+    load_order.start()
+    load_table.start()
     load_w.start()
 
     barrier = pltpu.get_barrier_semaphore()
@@ -63,8 +67,8 @@
 
     square = chips == 4
     chip_x, chip_y = chip % 2, chip // 2
-    xn = (chip_y * 2 + 1 - chip_x) * 2 + core
-    yn = ((1 - chip_y) * 2 + chip_x) * 2 + core
+    xn = (chip_y * 2 + 1 - chip_x) * 2 + 1 - core
+    yn = ((1 - chip_y) * 2 + chip_x) * 2 + 1 - core
     dn = ((1 - chip_y) * 2 + 1 - chip_x) * 2 + core
     line = tp == 4
     side = mt // 2
@@ -120,7 +124,6 @@
     else:
         each(1, chips, send_all)
 
-    my_stretch = order[me]
     load_q.wait()
     for h in range(q_heads):
         q_rows[h * rows:(h + 1) * rows, :] = q_in[:, h * HEAD:(h + 1) * HEAD]
@@ -130,31 +133,37 @@
         seen = jnp.logical_and(key_stretch < my_stretch, table[my_stretch, key_stretch] == 1)
         return jnp.where(seen, 0.0, MASKED).astype(jnp.float32)
 
-    lane = lax.broadcasted_iota(jnp.int32, (1, 2 * rows), 1)
+    load_order.wait()
+    load_table.wait()
+    my_stretch = order[me]
     scale = LOG2E / HEAD**0.5
 
-    def attend(first_slot, count, first):
-        if count == 2:
-            bias = jnp.where(lane < rows, bias_of(first_slot), bias_of(first_slot + 1))
-        else:
-            bias = bias_of(first_slot)
-        start = pl.multiple_of(first_slot * rows, rows)
+    def attend(slots, first=False):
+        count = len(slots)
+
+        def rows_of(buf, cols):
+            return jnp.concatenate(
+                [buf[pl.ds(pl.multiple_of(s * rows, rows), rows), cols] for s in slots], axis=0
+            )
+
+        bias = jnp.concatenate(
+            [jnp.full((1, rows), bias_of(s), jnp.float32) for s in slots], axis=1
+        )
         for g in range(kv_heads):
             cols = slice(g * HEAD, (g + 1) * HEAD)
             here = slice(g * grows, (g + 1) * grows)
-            keys = k_buf[pl.ds(start, count * rows), cols]
-            values = v_buf[pl.ds(start, count * rows), cols]
+            keys = rows_of(k_buf, cols)
+            values = rows_of(v_buf, cols)
             scores = lax.dot_general(
                 q_rows[here, :], keys, (((1,), (1,)), ((), ())),
                 preferred_element_type=jnp.float32,
             )
             if first:
-                q_pos = lax.broadcasted_iota(jnp.int32, (grows, 2 * rows), 0) % rows
-                k_col = lax.broadcasted_iota(jnp.int32, (grows, 2 * rows), 1)
-                k_pos = k_col - core * rows
-                own = (k_pos >= 0) & (k_pos < rows)
+                shape = (grows, count * rows)
+                q_pos = lax.broadcasted_iota(jnp.int32, shape, 0) % rows
+                k_pos = lax.broadcasted_iota(jnp.int32, shape, 1)
                 scores = jnp.where(
-                    own, jnp.where(k_pos <= q_pos, scores, MASKED), scores + bias
+                    k_pos < rows, jnp.where(k_pos <= q_pos, scores, MASKED), scores + bias
                 )
             else:
                 scores = scores + bias
@@ -178,7 +187,7 @@
         remote(v_buf, s, v_fwd, v_recv, 0, partner).wait_recv()
 
     wait_slot(partner)
-    attend(chip * 2, 2, True)
+    attend([me, partner], True)
 
     def step(j):
         s = ((chip - j + chips) % chips) * 2 + core
@@ -188,7 +197,7 @@
         remote(v_buf, s, v_fwd, v_recv, j, partner).wait_recv()
         remote(v_buf, s, v_fwd, v_recv, j, partner).start()
         wait_slot(other)
-        attend(s - core, 2, False)
+        attend([s, other])
 
     def arrive(buf, recv, fwd, s, j, onward=None, send=None):
         remote(buf, s, fwd, recv, j, partner).wait_recv()
@@ -201,15 +210,15 @@
         arrive(v_buf, v_recv, v_fwd, yn, 2, xn, v_send)
         arrive(v_buf, v_recv, v_fwd, xn, 1)
         arrive(k_buf, k_recv, k_fwd, yn, 2)
-        wait_slot(xn + 1 - 2 * core)
-        attend(xn - core, 2, False)
-        wait_slot(yn + 1 - 2 * core)
-        attend(yn - core, 2, False)
+        attend([xn, yn])
         arrive(k_buf, k_recv, k_fwd, dn, 3)
         arrive(v_buf, v_recv, v_fwd, dn, 3)
-        attend(dn, 1, False)
-        wait_slot(dn + 1 - 2 * core)
-        attend(dn + 1 - 2 * core, 1, False)
+        xo, yo, do = xn - 1 + 2 * core, yn - 1 + 2 * core, dn + 1 - 2 * core
+        wait_slot(xo)
+        wait_slot(yo)
+        attend([xo, yo, dn])
+        wait_slot(do)
+        attend([do])
     else:
         each(1, chips, step)
 
@@ -331,12 +340,14 @@
             in_specs=[
                 pl.BlockSpec(memory_space=pl.ANY),
                 pl.BlockSpec(memory_space=pl.ANY),
-                pl.BlockSpec(memory_space=pltpu.SMEM),
-                pl.BlockSpec(memory_space=pltpu.SMEM),
+                pl.BlockSpec(memory_space=pl.ANY),
+                pl.BlockSpec(memory_space=pl.ANY),
                 pl.BlockSpec(memory_space=pl.ANY),
             ],
             out_specs=pl.BlockSpec(memory_space=pltpu.VMEM),
             scratch_shapes=[
+                pltpu.SMEM(stretch_order.shape, jnp.int32),
+                pltpu.SMEM(block_table.shape, jnp.int32),
                 pltpu.VMEM((rows, q_width), jnp.bfloat16),
                 pltpu.VMEM((q_heads * rows, HEAD), jnp.bfloat16),
                 pltpu.VMEM((n * rows, kv_width), jnp.bfloat16),
@@ -348,13 +359,15 @@
                 pltpu.VMEM((tp, rows, dout // tp), jnp.bfloat16),
                 pltpu.VMEM((tp, rows, dout // tp), jnp.bfloat16),
                 pltpu.VMEM((rows, dout // tp), jnp.bfloat16),
-                dma((4,)),
+                dma((6,)),
                 dma((n // 2,)), dma((n // 2,)),
                 dma((n,)), dma((n,)),
                 dma((n // 2,)), dma((n // 2,)),
                 dma((max(tp, 4),)), dma((tp,)), dma((2,)),
             ],
-            compiler_params=pltpu.CompilerParams(collective_id=0, has_side_effects=True),
+            compiler_params=pltpu.CompilerParams(
+                collective_id=0, has_side_effects=True,
+            ),
         )(queries, keyvalues, stretch_order, block_table, proj_weight)
 
     return jax.shard_map(

time: 31.5 us -> 28 us (0.89)
  Pallas kernels: 29.7 us -> 26.3 us
    pallas_call x1, Pallas kernels: 29.7 us -> 26.3 us  [per_device(): pl.pallas_call(functools.partial(kernel, n, tp), out_shape=jax.ShapeDtype...]
where the time goes in v3:
time: 28 us; the launch traced here: 27.9 us
  Pallas kernels  26.3 us (94%)
  local copies, waits for them, and re-layouts  1.57 us (6%)
    pallas_call x1, Pallas kernels, per_device(): pl.pallas_call(functools.partial(kernel, n, tp), out_shape=jax.ShapeDtype...  26.3 us
    unnamed x1, local copies, waits for them, and re-layouts  1.57 us

profile of v3, /device:TPU:0, one launch (start us, length us, event | category | flops | bytes accessed | tf_op | source)
XLA Modules:
  0.0 27.9 jit_solution(4328347621015976401)
XLA Ops:
  0.0 26.3 %shard_map.55 = bf16[128,512]{1,0:T(8,128)(2,1)} custom-call(bf16[128,1024]{1,0:T(8,128)(2,1)} %q_hbm.1, bf16[2,128,256]{2,1,0:T(8,128)(2,1)} %kv_hbm.1, s32[8]{0:T(128)} %order_hbm.1, s32[8,8]{1,0:T(8,128)} %table_hbm.1, bf16[1024,2048]{1,0:T(8,128)(2,1)} %w_hbm.1), custom_call_target="tpu_custom_call" | custom-call | tf_op jit(solution)/shard_map/pallas_call | solution.py:337
  26.3 1.6 %copy.7 = bf16[128,512]{1,0:T(8,128)(2,1)} copy(bf16[128,512]{1,0:T(8,128)(2,1)} %shard_map.55) | data formatting | bytes 262144

commit v4 on v3

--- a/solution.py
+++ b/solution.py
@@ -243,8 +243,8 @@
             device_id={"tp": target}, device_id_type=MESH,
         )
 
-    def half_copy(i, dst, recv, target):
-        piece = pl.ds(i * (rows // 2), rows // 2)
+    def piece_copy(i, dst, recv, target):
+        piece = pl.ds(i * (rows // 4), rows // 4)
         return pltpu.make_async_remote_copy(
             src_ref=parts.at[2, piece], dst_ref=dst.at[piece],
             send_sem=p_send.at[2 + i], recv_sem=recv,
@@ -257,8 +257,8 @@
         @pl.when(inner == 0)
         def _():
             parts[2] = project(m3).astype(jnp.bfloat16)
-            for i in range(2):
-                half_copy(i, relay, r_recv.at[i], m1).start()
+            for i in range(4):
+                piece_copy(i, relay, r_recv.at[i], m1).start()
             parts[0] = project(m2).astype(jnp.bfloat16)
             part_copy(0, mt, m2).start()
             parts[1] = project(m1).astype(jnp.bfloat16)
@@ -266,8 +266,8 @@
             total = project(mt)
             part_copy(0, m1, m1).wait_recv()
             total = total + got[m1].astype(jnp.float32)
-            for i in range(2):
-                half_copy(i, got.at[m2], r_recv.at[i], m2).wait_recv()
+            for i in range(4):
+                piece_copy(i, got.at[m2], r_recv.at[i], m2).wait_recv()
             total = total + got[m2].astype(jnp.float32)
             out_ref[...] = total.astype(out_ref.dtype)
 
@@ -279,11 +279,11 @@
             part_copy(1, mt, m0).start()
             far = project(m3)
             total = project(mt)
-            for i in range(2):
-                piece = slice(i * (rows // 2), (i + 1) * (rows // 2))
-                half_copy(i, relay, r_recv.at[i], m0).wait_recv()
+            for i in range(4):
+                piece = slice(i * (rows // 4), (i + 1) * (rows // 4))
+                piece_copy(i, relay, r_recv.at[i], m0).wait_recv()
                 parts[2, piece] = (far[piece] + relay[piece].astype(jnp.float32)).astype(jnp.bfloat16)
-                half_copy(i, got.at[mt], r_recv.at[i], m3).start()
+                piece_copy(i, got.at[mt], r_recv.at[i], m3).start()
             for source in (m2, m3, m0):
                 part_copy(0, source, source).wait_recv()
                 total = total + got[source].astype(jnp.float32)
@@ -291,8 +291,8 @@
 
         part_copy(0, mt, m2).wait_send()
         part_copy(1, mt, m0).wait_send()
-        for i in range(2):
-            half_copy(i, relay, r_recv.at[i], m1).wait_send()
+        for i in range(4):
+            piece_copy(i, relay, r_recv.at[i], m1).wait_send()
     else:
         ahead = sorted(range(1, tp), key=lambda j: -min(j, tp - j))
         for j in ahead:
@@ -363,7 +363,7 @@
                 dma((n // 2,)), dma((n // 2,)),
                 dma((n,)), dma((n,)),
                 dma((n // 2,)), dma((n // 2,)),
-                dma((max(tp, 4),)), dma((tp,)), dma((2,)),
+                dma((max(tp, 6),)), dma((tp,)), dma((4,)),
             ],
             compiler_params=pltpu.CompilerParams(
                 collective_id=0, has_side_effects=True,

time: 28 us -> 27.7 us (0.989)
  Pallas kernels: 26.3 us -> 26 us
    pallas_call x1, Pallas kernels: 26.3 us -> 26 us  [per_device(): pl.pallas_call(functools.partial(kernel, n, tp), out_shape=jax.ShapeDtype...]
where the time goes in v4:
time: 27.7 us; the launch traced here: 27.5 us
  Pallas kernels  26 us (94%)
  local copies, waits for them, and re-layouts  1.57 us (6%)
    pallas_call x1, Pallas kernels, per_device(): pl.pallas_call(functools.partial(kernel, n, tp), out_shape=jax.ShapeDtype...  26 us
    unnamed x1, local copies, waits for them, and re-layouts  1.57 us

profile of v4, /device:TPU:0, one launch (start us, length us, event | category | flops | bytes accessed | tf_op | source)
XLA Modules:
  0.0 27.5 jit_solution(14394305282401916820)
XLA Ops:
  0.0 26.0 %shard_map.55 = bf16[128,512]{1,0:T(8,128)(2,1)} custom-call(bf16[128,1024]{1,0:T(8,128)(2,1)} %q_hbm.1, bf16[2,128,256]{2,1,0:T(8,128)(2,1)} %kv_hbm.1, s32[8]{0:T(128)} %order_hbm.1, s32[8,8]{1,0:T(8,128)} %table_hbm.1, bf16[1024,2048]{1,0:T(8,128)(2,1)} %w_hbm.1), custom_call_target="tpu_custom_call" | custom-call | tf_op jit(solution)/shard_map/pallas_call | solution.py:337
  26.0 1.6 %copy.7 = bf16[128,512]{1,0:T(8,128)(2,1)} copy(bf16[128,512]{1,0:T(8,128)(2,1)} %shard_map.55) | data formatting | bytes 262144
